TPU v7x, 32 devices: a whole 2x2x4 slice. The times are simulated.
32 devices in a mesh: group: 2 (over x), row: 4 (over y, core), col: 4 (over z).
Axes of the slice: x: 2, y: 2, z: 4, core: 2. Of those that a mesh axis runs over, the one named last changes fastest.
Arguments:
- pair_repr: bfloat16 [128, 128, 128], P(('group', 'row'), 'col'), may hold values from -6 to 6
- pair_mask: int32 [128, 128], P(('group', 'row'), 'col'), may hold values 0 or 1
- chain_id: int32 [128], replicated, may hold values from 0 to 7, never falling along the last dimension, each value on 1 to 32 neighbouring positions
- tri_in_gain: float32 [128], replicated, may hold values from 0.5 to 1.5
- tri_proj: bfloat16 [128, 512], replicated, may hold values from -0.5 to 0.5
- tri_gate: bfloat16 [128, 128], replicated, may hold values from -0.5 to 0.5
- tri_out_gain: float32 [128], replicated, may hold values from 0.5 to 1.5
- tri_out: bfloat16 [128, 128], replicated, may hold values from -0.5 to 0.5
- bias_gain: float32 [128], replicated, may hold values from 0.5 to 1.5
- bias_weight: bfloat16 [128, 16], replicated, may hold values from -0.5 to 0.5
- chain_bias: float32 [16], replicated, may hold values from -2 to 2
- tokens: bfloat16 [24, 128, 768], P(('group', 'row')), may hold values from -6 to 6
- noise_level: int32 [24], P(('group', 'row')), may hold values from 0 to 199
- attn_gain: float32 [768], replicated, may hold values from 0.5 to 1.5
- attn_weight: bfloat16 [4, 768, 768], P(None, None, 'col'), may hold values from -0.21875 to 0.21875
- out_weight: bfloat16 [768, 768], P('col'), may hold values from -0.21875 to 0.21875
- cotangent: bfloat16 [24, 128, 768], P(('group', 'row')), may hold values from -6 to 6
Outputs:
- pair_next: bfloat16 [128, 128, 128], P(('group', 'row'), 'col')
- pair_grad: float32 [128, 128, 128], P(('group', 'row'), 'col')
- bias_weight_grad: float32 [128, 16], replicated
- denoised: bfloat16 [24, 128, 768], P(('group', 'row'), 'col')
- token_grad: bfloat16 [24, 128, 768], P(('group', 'row'), 'col')
- attn_weight_grad: float32 [4, 768, 768], P(None, ('group', 'row'), 'col')
- out_weight_grad: float32 [768, 768], P('col', ('group', 'row'))
Inputs may be any that keep to these rules, and one draw needn't show every extreme that they name: `chain_id`: chain numbers never fall along the tokens.
All inputs are finite; a program needn't handle non-finite values. No bound on the sum of `pair_mask` on one device may be relied on, other than what follows from the above.
Results may differ from a plain program's by a relative error of at most 0.014.
Values may be sent and summed in bfloat16 or wider, within the bound.
No kernel may reach another device: no remote copies, remote signals or barrier semaphores. Data moves between devices by JAX's collectives and lax.ppermute only.
A program may use at most 64 MiB of HBM per device.

v0:
```python
import math
import jax
import jax.numpy as jnp
from jax import lax
from jax.sharding import PartitionSpec as P

LEVELS = 200
EPSILON = 1e-05
SIGMA_LOW = 0.1
SIGMA_SPAN = 100.0


def normalize(values):
    average = jnp.mean(values, -1, keepdims=True)
    centred = values - average
    return centred * lax.rsqrt(jnp.mean(centred * centred, -1, keepdims=True) + EPSILON)


def norm_back(gradient, values, norm_gain):
    average = jnp.mean(values, -1, keepdims=True)
    centred = values - average
    inverse = lax.rsqrt(jnp.mean(centred * centred, -1, keepdims=True) + EPSILON)
    normed = centred * inverse
    weighted = gradient * norm_gain
    return inverse * (
        weighted
        - jnp.mean(weighted, -1, keepdims=True)
        - normed * jnp.mean(weighted * normed, -1, keepdims=True)
    )


def noise_scale(levels):
    sigma_vals = SIGMA_LOW * SIGMA_SPAN ** (levels.astype(jnp.float32) / (LEVELS - 1))
    return lax.rsqrt(1.0 + sigma_vals * sigma_vals)


def shards(
    pair_repr,
    pair_mask,
    chain_id,
    tri_in_gain,
    tri_proj,
    tri_gate,
    tri_out_gain,
    tri_out,
    bias_gain,
    bias_weight,
    chain_bias,
    tokens,
    noise_level,
    attn_gain,
    attn_weight,
    out_weight,
    cotangent,
):
    rows_here = pair_repr.shape[0]
    cols_here = pair_repr.shape[1]
    channels = pair_repr.shape[2]
    token_count = chain_id.shape[0]
    heads_all = bias_weight.shape[1]
    hidden_width = attn_gain.shape[0]
    head_size = hidden_width // heads_all
    inverse_square_root = 1.0 / math.sqrt(head_size)
    row_index = lax.axis_index(("group", "row"))
    col_index = lax.axis_index("col")
    pair_tile = pair_repr.astype(jnp.float32)
    pair_in = (normalize(pair_tile) * tri_in_gain).astype(jnp.bfloat16)
    flat_in = pair_in.reshape(-1, channels)
    projected = jnp.dot(flat_in, tri_proj, preferred_element_type=jnp.float32).reshape(
        rows_here, cols_here, 4, channels
    )
    mask_tile = pair_mask.astype(jnp.float32)[:, :, None]
    left_proj = (jax.nn.sigmoid(projected[:, :, 0]) * projected[:, :, 1] * mask_tile).astype(
        jnp.bfloat16
    )
    right_proj = (jax.nn.sigmoid(projected[:, :, 2]) * projected[:, :, 3] * mask_tile).astype(
        jnp.bfloat16
    )
    gate_act = jax.nn.sigmoid(
        jnp.dot(flat_in, tri_gate, preferred_element_type=jnp.float32)
    ).reshape(rows_here, cols_here, channels)
    left_major = jnp.transpose(left_proj, (2, 0, 1))
    right_major = jnp.transpose(right_proj, (2, 0, 1))
    partial_rows = jnp.einsum(
        "cjk,cik->cji",
        lax.all_gather(right_major, ("group", "row"), axis=1, tiled=True),
        left_major,
        preferred_element_type=jnp.float32,
    )
    summed = lax.psum_scatter(partial_rows, "col", scatter_dimension=1, tiled=True)
    triangle = jnp.transpose(summed, (2, 1, 0))
    tri_normed = (normalize(triangle) * tri_out_gain).astype(jnp.bfloat16)
    update = jnp.dot(
        tri_normed.reshape(-1, channels), tri_out, preferred_element_type=jnp.float32
    ).reshape(rows_here, cols_here, channels)
    updated = pair_tile + gate_act * update
    bias_in = (normalize(updated) * bias_gain).astype(jnp.bfloat16)
    flat_bias = bias_in.reshape(-1, channels)
    bias_tile = jnp.dot(flat_bias, bias_weight, preferred_element_type=jnp.float32).reshape(
        rows_here, cols_here, heads_all
    )
    row_chain = lax.dynamic_slice_in_dim(chain_id, row_index * rows_here, rows_here)
    col_chain = lax.dynamic_slice_in_dim(chain_id, col_index * cols_here, cols_here)
    same_chain = (row_chain[:, None] == col_chain[None, :]).astype(jnp.float32)
    bias_tile = bias_tile + same_chain[:, :, None] * chain_bias
    bias_major = jnp.transpose(bias_tile.astype(jnp.bfloat16), (2, 0, 1))
    head_rows = lax.all_to_all(bias_major, "col", split_axis=0, concat_axis=2, tiled=True)
    per_head_bias = lax.all_gather(head_rows, ("group", "row"), axis=1, tiled=True).astype(
        jnp.float32
    )
    local_heads = per_head_bias.shape[0]
    scales = noise_scale(noise_level)

    def one_copy(carried, inputs):
        bias_sums, weight_sums, output_sums = carried
        token_rows, cot_rows, scaling = inputs
        sequence_length = token_rows.shape[0]
        scaled = scaling * token_rows.astype(jnp.float32)
        hidden = (normalize(scaled) * attn_gain).astype(jnp.bfloat16)
        projections = jnp.einsum(
            "nd,gde->gne", hidden, attn_weight, preferred_element_type=jnp.float32
        )
        query_rows = (
            projections[0].astype(jnp.bfloat16).reshape(sequence_length, local_heads, head_size)
        )
        key_matrix = (
            projections[1].astype(jnp.bfloat16).reshape(sequence_length, local_heads, head_size)
        )
        value_rows = (
            projections[2].astype(jnp.bfloat16).reshape(sequence_length, local_heads, head_size)
        )
        gate_sig = jax.nn.sigmoid(projections[3])
        logit_scores = (
            jnp.einsum("fuc,suc->ufs", query_rows, key_matrix, preferred_element_type=jnp.float32)
            * inverse_square_root
            + per_head_bias
        )
        exponent = jnp.exp(logit_scores)
        attention = exponent / jnp.sum(exponent, -1, keepdims=True)
        attention_probs = attention.astype(jnp.bfloat16)
        attended_rows = jnp.einsum(
            "vkq,qvy->kvy", attention_probs, value_rows, preferred_element_type=jnp.float32
        ).reshape(sequence_length, -1)
        gated_out = (gate_sig * attended_rows).astype(jnp.bfloat16)
        grad_gated = jnp.dot(cot_rows, out_weight.T, preferred_element_type=jnp.float32)
        grad_gate = grad_gated * attended_rows * gate_sig * (1.0 - gate_sig)
        attended_gradient = (
            (grad_gated * gate_sig)
            .astype(jnp.bfloat16)
            .reshape(sequence_length, local_heads, head_size)
        )
        probability_gradient = jnp.einsum(
            "fuc,suc->ufs", attended_gradient, value_rows, preferred_element_type=jnp.float32
        )
        value_gradient = jnp.einsum(
            "avj,vat->jat", attention_probs, attended_gradient, preferred_element_type=jnp.float32
        )
        grad_score = attention * (
            probability_gradient - jnp.sum(attention * probability_gradient, -1, keepdims=True)
        )
        score_gradient = grad_score.astype(jnp.bfloat16)
        query_gradient = (
            jnp.einsum(
                "vkq,qvy->kvy", score_gradient, key_matrix, preferred_element_type=jnp.float32
            )
            * inverse_square_root
        )
        key_gradient = (
            jnp.einsum(
                "avj,vat->jat", score_gradient, query_rows, preferred_element_type=jnp.float32
            )
            * inverse_square_root
        )
        grads = jnp.stack(
            [
                query_gradient.reshape(sequence_length, -1),
                key_gradient.reshape(sequence_length, -1),
                value_gradient.reshape(sequence_length, -1),
                grad_gate,
            ]
        ).astype(jnp.bfloat16)
        weight_sums = weight_sums + jnp.einsum(
            "nd,gne->gde", hidden, grads, preferred_element_type=jnp.float32
        )
        output_sums = output_sums + jnp.dot(
            gated_out.T, cot_rows, preferred_element_type=jnp.float32
        )
        return ((bias_sums + grad_score, weight_sums, output_sums), (gated_out, grads))

    start_sums = (
        jnp.zeros((local_heads, token_count, token_count), jnp.float32),
        jnp.zeros(attn_weight.shape, jnp.float32),
        jnp.zeros(out_weight.shape, jnp.float32),
    )
    final_sums, stacked = lax.scan(one_copy, start_sums, (tokens, cotangent, scales))
    bias_sums, weight_sums, output_sums = final_sums
    gated_all, grads_all = stacked
    token_share = token_count // lax.axis_size("col")
    attn_parts = jnp.einsum(
        "tnd,de->tne", gated_all, out_weight, preferred_element_type=jnp.float32
    )
    hidden_parts = jnp.einsum(
        "tgne,gde->tnd", grads_all, attn_weight, preferred_element_type=jnp.float32
    )
    attn_out, grad_hidden = (
        lax.psum_scatter(attn_parts, "col", scatter_dimension=1, tiled=True),
        lax.psum_scatter(hidden_parts, "col", scatter_dimension=1, tiled=True),
    )
    first_token = col_index * token_share
    token_mine = lax.dynamic_slice_in_dim(tokens, first_token, token_share, 1)
    cot_mine = lax.dynamic_slice_in_dim(cotangent, first_token, token_share, 1)
    scaled_mine = scales[:, None, None] * token_mine.astype(jnp.float32)
    denoised = (scaled_mine + attn_out).astype(jnp.bfloat16)
    grad_scaled = cot_mine.astype(jnp.float32) + norm_back(grad_hidden, scaled_mine, attn_gain)
    token_grad = (scales[:, None, None] * grad_scaled).astype(jnp.bfloat16)
    bias_rows_sum, out_grad, weight_grad = (
        lax.psum_scatter(bias_sums, ("group", "row"), scatter_dimension=1, tiled=True),
        lax.psum_scatter(output_sums, ("group", "row"), scatter_dimension=1, tiled=True),
        lax.psum_scatter(weight_sums, ("group", "row"), scatter_dimension=1, tiled=True),
    )
    bias_back = lax.all_to_all(bias_rows_sum, "col", split_axis=2, concat_axis=0, tiled=True)
    grad_bias = jnp.transpose(bias_back, (1, 2, 0)).reshape(-1, heads_all)
    grad_in = jnp.dot(
        grad_bias, bias_weight.astype(jnp.float32).T, precision=lax.Precision.HIGHEST
    ).reshape(rows_here, cols_here, channels)
    pair_grad = norm_back(grad_in, updated, bias_gain)
    weight_part = jnp.dot(
        flat_bias.astype(jnp.float32).T, grad_bias, precision=lax.Precision.HIGHEST
    )
    bias_weight_grad = lax.psum(weight_part, ("group", "row", "col"))
    return (
        updated.astype(jnp.bfloat16),
        pair_grad,
        bias_weight_grad,
        denoised,
        token_grad,
        weight_grad,
        out_grad,
    )


def solution(mesh):
    return jax.shard_map(
        shards,
        mesh=mesh,
        in_specs=(
            P(("group", "row"), "col", None),
            P(("group", "row"), "col"),
            P(),
            P(),
            P(),
            P(),
            P(),
            P(),
            P(),
            P(),
            P(),
            P(("group", "row"), None, None),
            P(("group", "row")),
            P(),
            P(None, None, "col"),
            P("col", None),
            P(("group", "row"), None, None),
        ),
        out_specs=(
            P(("group", "row"), "col", None),
            P(("group", "row"), "col", None),
            P(),
            P(("group", "row"), "col", None),
            P(("group", "row"), "col", None),
            P(None, ("group", "row"), "col"),
            P("col", ("group", "row")),
        ),
        check_vma=False,
    )
```

profile of v0, /device:TPU:0, one launch (start us, length us, event | category | flops | bytes accessed | tf_op | source)
XLA Modules:
  0.0 379.4 jit_solution(1215166958934254684)
XLA Ops:
  14.0 25.8 %all-gather.2.cloned.1.call-done = bf16[128,128,32]{0,2,1:T(8,128)(2,1)} async-done(((bf16[128,16,32]{0,2,1:T(8,128)(2,1)}), bf16[128,128,32]{0,2,1:T(8,128)(2,1)}) %all-gather.2.cloned.1.call-update) | async-done | bytes 1048592 | tf_op jit(solution)/shard_map/all_gather | solution.py:86
  39.7 7.3 %copy.96 = bf16[128,128,32]{2,1,0:T(8,128)(2,1)} copy(bf16[128,128,32]{0,2,1:T(8,128)(2,1)} %all-gather.2.cloned.1.call-done) | data formatting | bytes 2097152 | tf_op jit(solution)/shard_map/all_gather | solution.py:86
  47.0 4.4 %fusion.84 = f32[128,128,16]{1,2,0:T(8,128)S(1)} fusion(bf16[128,128,32]{2,1,0:T(8,128)(2,1)} %copy.96, bf16[128,16,32]{2,1,0:T(8,128)(2,1)S(1)} %copy.97), kind=kOutput, calls=%fused_computation.149 | convolution fusion | flops 16777216 | bytes 2228224 | tf_op jit(solution)/shard_map/cjk,cik->cji/dot_general | solution.py:84
  53.6 27.0 %reduce-scatter.8.cloned.1.call-done = f32[128,32,16]{0,2,1:T(8,128)} async-done(((f32[128,128,16]{0,2,1:T(8,128)}), f32[128,32,16]{0,2,1:T(8,128)}) %reduce-scatter.8.cloned.1.call-update) | async-done | bytes 262160 | tf_op jit(solution)/shard_map/reduce_scatter | solution.py:90
  86.5 3.3 all-to-all-start
  89.8 5.5 %all-to-all-done = bf16[4,2,1024]{2,1,0:T(2,128)(2,1)S(1)} async-done(((bf16[4,2,1024]{2,1,0:T(2,128)(2,1)}), bf16[4,2,1024]{2,1,0:T(2,128)(2,1)S(1)}, u32[]{:S(2)}, u32[]{:S(2)}) %all-to-all-start) | async-done | bytes 16416 | tf_op jit(solution)/shard_map/all_to_all | solution.py:107
  95.6 9.2 %all_gather.7 = bf16[4,128,128]{2,0,1:T(4,128)(2,1)S(1)} all-gather(bf16[4,16,128]{2,0,1:T(4,128)(2,1)S(1)} %all_to_all.29), channel_id=1, replica_groups=mesh['group'=2,'row'=4,'col'=4] {'group','row'}, dimensions={1}, use_global_device_ids=true | all-gather | bytes 147456 | tf_op jit(solution)/shard_map/all_gather | solution.py:108
  105.6 66.1 %while.19 = (s32[]{:T(128)}, f32[4,128,128]{1,2,0:T(8,128)}, f32[4,768,192]{1,2,0:T(8,128)S(1)}, f32[192,768]{1,0:T(8,128)}, bf16[3,128,192]{1,2,0:T(8,128)(2,1)...) while((s32[]{:T(128)}, f32[4,128,128]{1,2,0:T(8,128)}, ...), condition=%wide.region_12.13_spmd.clone, body=%wide.region_7.12_spmd.clone.sunk | while | flops 421316096 | bytes 18337588 | solution.py:195
  107.5 2.4 fusion.165
  122.5 2.2 bitcast_add_fusion.2
  129.3 2.4 fusion.165
  144.4 2.2 bitcast_add_fusion.2
  151.5 2.4 fusion.165
  173.5 2.3 copy.118
  175.9 3.2 convolution_bitcast_fusion
  179.1 2.3 fusion.48
  181.5 2.3 copy.110
  186.1 38.7 %all-reduce.3.cloned.1.call-done = f32[4,128,128]{2,0,1:T(4,128)} async-done(((f32[4,128,128]{2,0,1:T(4,128)}), f32[4,128,128]{2,0,1:T(4,128)}) %all-reduce.3.cloned.1.call-update) | async-done | bytes 262160
  226.6 4.6 %all-to-all-start.1 = ((f32[4,1,2048]{2,1,0:T(1,128)}), f32[4,1,2048]{2,1,0:T(1,128)S(1)}, u32[]{:S(2)}, u32[]{:S(2)}) async-start(f32[4,1,2048]{2,1,0:T(1,128)} %reshape.298), calls=%async_computation.2 | async-start | bytes 65536 | tf_op jit(solution)/shard_map/all_to_all | solution.py:221
  231.2 5.7 %all-to-all-done.1 = f32[4,1,2048]{2,1,0:T(1,128)S(1)} async-done(((f32[4,1,2048]{2,1,0:T(1,128)}), f32[4,1,2048]{2,1,0:T(1,128)S(1)}, u32[]{:S(2)}, u32[]{:S(2)}) %all-to-all-start.1) | async-done | bytes 32800 | tf_op jit(solution)/shard_map/all_to_all | solution.py:221
  238.9 38.5 %psum.7 = f32[128,16]{0,1:T(8,128)} all-reduce(f32[128,16]{0,1:T(8,128)S(1)} %convolution_bitcast_fusion.2), channel_id=1, replica_groups=mesh['group'=2,'row'=4,'col'=4] {'group','row','col'}, use_global_device_ids=true, to_apply=%region_16.17 | all-reduce | flops 2048 | bytes 16384 | tf_op jit(solution)/shard_map/psum | solution.py:230
  280.6 13.2 %reduce-scatter.12.cloned.1.call-done = f32[3,32,768]{2,1,0:T(8,128)} async-done(((f32[3,128,768]{2,1,0:T(8,128)}), f32[3,32,768]{2,1,0:T(8,128)}) %reduce-scatter.12.cloned.1.call-update) | async-done | bytes 294928 | tf_op jit(solution)/shard_map/reduce_scatter | solution.py:207
  295.0 29.0 %reduce-scatter.10.cloned.1.call-done = f32[3,32,768]{2,1,0:T(8,128)} async-done(((f32[3,128,768]{2,1,0:T(8,128)}), f32[3,32,768]{2,1,0:T(8,128)}) %reduce-scatter.10.cloned.1.call-update) | async-done | bytes 294928 | tf_op jit(solution)/shard_map/reduce_scatter | solution.py:206
  325.9 46.6 %reduce-scatter.14.cloned.1.call-done = f32[4,96,192]{2,1,0:T(8,128)} async-done(((f32[4,768,192]{2,1,0:T(8,128)}), f32[4,96,192]{2,1,0:T(8,128)}) %reduce-scatter.14.cloned.1.call-update) | async-done | bytes 294928 | tf_op jit(solution)/shard_map/reduce_scatter | solution.py:219
  (199 shorter events, 83.8 us)
Async XLA Ops:
  7.2 77.1 %copy-start = (bf16[128,128]{1,0:T(8,128)(2,1)S(1)}, bf16[128,128]{1,0:T(8,128)(2,1)}, u32[]{:S(2)}) copy-start(bf16[128,128]{1,0:T(8,128)(2,1)} %param.26) | copy-start | bytes 98308
  7.2 32.5 %all-gather.2.cloned.1.call-start = ((), (), s32[]{:S(2)}) async-start(), calls=%async_computation.7 | async-start | bytes 1179648 | tf_op jit(solution)/shard_map/all_gather | solution.py:86
  13.5 67.1 %reduce-scatter.8.cloned.1.call-start = ((), (), s32[]{:S(2)}) async-start(), calls=%async_computation.8 | async-start | bytes 1310720 | tf_op jit(solution)/shard_map/reduce_scatter | solution.py:90
  51.4 31.7 %copy-start.15 = (f32[128]{0:T(128)S(1)}, f32[128]{0:T(128)}, u32[]{:S(2)}) copy-start(f32[128]{0:T(128)} %param.25) | copy-start | bytes 1540
  51.4 32.9 %copy-start.7 = (bf16[16,32,128]{2,1,0:T(8,128)(2,1)S(1)}, bf16[16,32,128]{2,1,0:T(8,128)(2,1)}, u32[]{:S(2)}) copy-start(bf16[16,32,128]{2,1,0:T(8,128)(2,1)} %param.19) | copy-start | bytes 393220
  53.1 32.3 %copy-start.11 = (bf16[128,16]{0,1:T(8,128)(2,1)S(1)}, bf16[128,16]{0,1:T(8,128)(2,1)}, u32[]{:S(2)}) copy-start(bf16[128,16]{0,1:T(8,128)(2,1)} %param.28) | copy-start | bytes 12292
  53.1 32.3 %copy-start.13 = (f32[128]{0:T(128)S(1)}, f32[128]{0:T(128)}, u32[]{:S(2)}) copy-start(f32[128]{0:T(128)} %param.27) | copy-start | bytes 1540
  53.1 32.3 %copy-start.18 = (f32[16]{0:T(128)S(1)}, f32[16]{0:T(128)}, u32[]{:S(2)}) copy-start(f32[16]{0:T(128)} %param.29) | copy-start | bytes 196
  53.1 36.7 %copy-start.19 = (s32[3]{0:T(128)S(1)}, s32[3]{0:T(128)}, u32[]{:S(2)}) copy-start(s32[3]{0:T(128)} %param.31) | copy-start | bytes 40
  53.3 52.2 %copy-start.1 = (bf16[3,128,768]{2,1,0:T(8,128)(2,1)S(1)}, bf16[3,128,768]{2,1,0:T(8,128)(2,1)}, u32[]{:S(2)}) copy-start(bf16[3,128,768]{2,1,0:T(8,128)(2,1)} %param.30) | copy-start | bytes 1769476
  53.3 52.2 %copy-start.9 = (f32[768]{0:T(1024)S(1)}, f32[768]{0:T(1024)}, u32[]{:S(2)}) copy-start(f32[768]{0:T(1024)} %param.32) | copy-start | bytes 9220
  86.5 8.8 %all-to-all-start = ((bf16[4,2,1024]{2,1,0:T(2,128)(2,1)}), bf16[4,2,1024]{2,1,0:T(2,128)(2,1)S(1)}, u32[]{:S(2)}, u32[]{:S(2)}) async-start(bf16[4,2,1024]{2,1,0:T(2,128)(2,1)} %reshape.296), calls=%async_computation.1 | async-start | bytes 32768 | tf_op jit(solution)/shard_map/all_to_all | solution.py:107
  89.7 135.1 %all-reduce.3.cloned.1.call-start = ((), (), s32[]{:S(2)}) async-start(), calls=%async_computation.13 | async-start | bytes 524288
  105.6 4.4 %copy-start.4 = (f32[4,128,128]{1,2,0:T(8,128)S(1)}, f32[4,128,128]{1,2,0:T(8,128)}, u32[]{:S(2)}) copy-start(f32[4,128,128]{1,2,0:T(8,128)} %get-tuple-element.359) | copy-start | bytes 786436 | tf_op jit(solution)/shard_map/while
  127.4 4.4 %copy-start.4 = (f32[4,128,128]{1,2,0:T(8,128)S(1)}, f32[4,128,128]{1,2,0:T(8,128)}, u32[]{:S(2)}) copy-start(f32[4,128,128]{1,2,0:T(8,128)} %get-tuple-element.359) | copy-start | bytes 786436 | tf_op jit(solution)/shard_map/while
  149.5 4.4 %copy-start.4 = (f32[4,128,128]{1,2,0:T(8,128)S(1)}, f32[4,128,128]{1,2,0:T(8,128)}, u32[]{:S(2)}) copy-start(f32[4,128,128]{1,2,0:T(8,128)} %get-tuple-element.359) | copy-start | bytes 786436 | tf_op jit(solution)/shard_map/while
  173.5 105.5 %reduce-scatter.16.cloned.1.call-start = ((), (), s32[]{:S(2)}) async-start(), calls=%async_computation.12 | async-start | bytes 884736
  175.8 118.0 %reduce-scatter.12.cloned.1.call-start = ((), (), s32[]{:S(2)}) async-start(), calls=%async_computation.10 | async-start | bytes 1474560 | tf_op jit(solution)/shard_map/reduce_scatter | solution.py:207
  179.1 144.8 %reduce-scatter.10.cloned.1.call-start = ((), (), s32[]{:S(2)}) async-start(), calls=%async_computation.9 | async-start | bytes 1474560 | tf_op jit(solution)/shard_map/reduce_scatter | solution.py:206
  181.4 191.1 %reduce-scatter.14.cloned.1.call-start = ((), (), s32[]{:S(2)}) async-start(), calls=%async_computation.11 | async-start | bytes 3538944 | tf_op jit(solution)/shard_map/reduce_scatter | solution.py:219
  183.8 54.7 %copy-start.6 = (f32[16,32,128]{2,1,0:T(8,128)S(1)}, f32[16,32,128]{2,1,0:T(8,128)}, u32[]{:S(2)}) copy-start(f32[16,32,128]{2,1,0:T(8,128)} %copy-done.5) | copy-start | bytes 786436
  183.8 54.7 %copy-start.14 = (f32[128]{0:T(128)S(1)}, f32[128]{0:T(128)}, u32[]{:S(2)}) copy-start(f32[128]{0:T(128)} %param.27) | copy-start | bytes 1540
  183.8 93.5 %copy-start.12 = (bf16[128,16]{0,1:T(8,128)(2,1)S(1)}, bf16[128,16]{0,1:T(8,128)(2,1)}, u32[]{:S(2)}) copy-start(bf16[128,16]{0,1:T(8,128)(2,1)} %param.28) | copy-start | bytes 12292
  226.6 10.3 %all-to-all-start.1 = ((f32[4,1,2048]{2,1,0:T(1,128)}), f32[4,1,2048]{2,1,0:T(1,128)S(1)}, u32[]{:S(2)}, u32[]{:S(2)}) async-start(f32[4,1,2048]{2,1,0:T(1,128)} %reshape.298), calls=%async_computation.2 | async-start | bytes 65536 | tf_op jit(solution)/shard_map/all_to_all | solution.py:221
  (14 other events, 25.5 us)
Sparse Core Ops, SparseCore 0:
  13.6 26.0 all-gather.1
  53.2 27.2 reduce-scatter.7
  173.6 51.1 all-reduce.2
  227.8 34.3 reduce-scatter.15
  264.4 29.3 reduce-scatter.11
  296.0 27.9 reduce-scatter.9
  327.9 44.6 reduce-scatter.13
where the time goes:
time: 381 us; the launch traced here: 379 us
  waiting for transfers between devices  191 us (50%)
  matrix products  52.1 us (14%)
  blocking collectives  47.6 us (12%)
  other arithmetic  33.9 us (9%)
  local copies, waits for them, and re-layouts  30.6 us (8%)
  between operations  15.2 us (4%)
  starting transfers between devices  8.14 us (2%)
    reduce_scatter x1, waiting for transfers between devices, shards(): lax.psum_scatter(weight_sums, ('group', 'row'), scatter_dimension=1, tile...  46.6 us
    unnamed x9, waiting for transfers between devices  38.9 us
    psum x1, blocking collectives, shards(): bias_weight_grad = lax.psum(weight_part, ('group', 'row', 'col'))  38.5 us
    reduce_scatter x1, waiting for transfers between devices, shards(): lax.psum_scatter(attn_parts, 'col', scatter_dimension=1, tiled=True)  29 us
    reduce_scatter x1, waiting for transfers between devices, shards(): lax.psum_scatter(partial_rows, 'col', scatter_dimension=1, tiled=True)  27 us
    all_gather x1, waiting for transfers between devices, shards(): lax.all_gather(right_major, ('group', 'row'), axis=1, tiled=True)  25.8 us
    reduce_scatter x1, waiting for transfers between devices, shards(): lax.psum_scatter(hidden_parts, 'col', scatter_dimension=1, tiled=True)  13.2 us
    all_gather x1, blocking collectives, shards(): lax.all_gather(head_rows, ('group', 'row'), axis=1, tiled=True)  9.18 us
  transfers between devices with their start and end apart: 9, of which 8 were waited for; matrix products, arithmetic and copies ran while one was open for 6% of the time, Pallas kernels for 0%

commit v1 on v0

--- a/solution.py
+++ b/solution.py
@@ -227,7 +227,7 @@
     weight_part = jnp.dot(
         flat_bias.astype(jnp.float32).T, grad_bias, precision=lax.Precision.HIGHEST
     )
-    bias_weight_grad = lax.psum(weight_part, ("group", "row", "col"))
+    bias_weight_grad = lax.psum(lax.psum(weight_part, ("row", "col")), "group")
     return (
         updated.astype(jnp.bfloat16),
         pair_grad,

time: 381 us -> 381 us (level)
    psum x1 -> x2, blocking collectives: 38.5 us -> 36.8 us  [shards(): bias_weight_grad = lax.psum(lax.psum(weight_part, ('row', 'col')), 'group')]
where the time goes in v1:
time: 381 us; the launch traced here: 379 us
  waiting for transfers between devices  193 us (51%)
  matrix products  52.2 us (14%)
  blocking collectives  46 us (12%)
  other arithmetic  33.9 us (9%)
  local copies, waits for them, and re-layouts  30.6 us (8%)
  between operations  15.2 us (4%)
  starting transfers between devices  8.14 us (2%)
    reduce_scatter x1, waiting for transfers between devices, shards(): lax.psum_scatter(weight_sums, ('group', 'row'), scatter_dimension=1, tile...  46.6 us
    unnamed x9, waiting for transfers between devices  38.9 us
    psum x2, blocking collectives, shards(): bias_weight_grad = lax.psum(lax.psum(weight_part, ('row', 'col')), 'group')  36.8 us
    reduce_scatter x1, waiting for transfers between devices, shards(): lax.psum_scatter(attn_parts, 'col', scatter_dimension=1, tiled=True)  29 us
    reduce_scatter x1, waiting for transfers between devices, shards(): lax.psum_scatter(partial_rows, 'col', scatter_dimension=1, tiled=True)  27 us
    all_gather x1, waiting for transfers between devices, shards(): lax.all_gather(right_major, ('group', 'row'), axis=1, tiled=True)  25.8 us
    reduce_scatter x1, waiting for transfers between devices, shards(): lax.psum_scatter(hidden_parts, 'col', scatter_dimension=1, tiled=True)  14.8 us
    all_gather x1, blocking collectives, shards(): lax.all_gather(head_rows, ('group', 'row'), axis=1, tiled=True)  9.17 us
  transfers between devices with their start and end apart: 9, of which 8 were waited for; matrix products, arithmetic and copies ran while one was open for 6% of the time, Pallas kernels for 0%

profile of v1, /device:TPU:0, one launch (start us, length us, event | category | flops | bytes accessed | tf_op | source)
XLA Modules:
  0.0 379.4 jit_solution(13662844997040377966)
XLA Ops:
  14.0 25.8 %all-gather.2.cloned.1.call-done = bf16[128,128,32]{0,2,1:T(8,128)(2,1)} async-done(((bf16[128,16,32]{0,2,1:T(8,128)(2,1)}), bf16[128,128,32]{0,2,1:T(8,128)(2,1)}) %all-gather.2.cloned.1.call-update) | async-done | bytes 1048592 | tf_op jit(solution)/shard_map/all_gather | solution.py:86
  39.7 7.3 %copy.96 = bf16[128,128,32]{2,1,0:T(8,128)(2,1)} copy(bf16[128,128,32]{0,2,1:T(8,128)(2,1)} %all-gather.2.cloned.1.call-done) | data formatting | bytes 2097152 | tf_op jit(solution)/shard_map/all_gather | solution.py:86
  47.0 4.4 %fusion.84 = f32[128,128,16]{1,2,0:T(8,128)S(1)} fusion(bf16[128,128,32]{2,1,0:T(8,128)(2,1)} %copy.96, bf16[128,16,32]{2,1,0:T(8,128)(2,1)S(1)} %copy.97), kind=kOutput, calls=%fused_computation.149 | convolution fusion | flops 16777216 | bytes 2228224 | tf_op jit(solution)/shard_map/cjk,cik->cji/dot_general | solution.py:84
  53.6 27.0 %reduce-scatter.8.cloned.1.call-done = f32[128,32,16]{0,2,1:T(8,128)} async-done(((f32[128,128,16]{0,2,1:T(8,128)}), f32[128,32,16]{0,2,1:T(8,128)}) %reduce-scatter.8.cloned.1.call-update) | async-done | bytes 262160 | tf_op jit(solution)/shard_map/reduce_scatter | solution.py:90
  86.5 3.3 all-to-all-start
  89.8 5.5 %all-to-all-done = bf16[4,2,1024]{2,1,0:T(2,128)(2,1)S(1)} async-done(((bf16[4,2,1024]{2,1,0:T(2,128)(2,1)}), bf16[4,2,1024]{2,1,0:T(2,128)(2,1)S(1)}, u32[]{:S(2)}, u32[]{:S(2)}) %all-to-all-start) | async-done | bytes 16416 | tf_op jit(solution)/shard_map/all_to_all | solution.py:107
  95.6 9.2 %all_gather.7 = bf16[4,128,128]{2,0,1:T(4,128)(2,1)S(1)} all-gather(bf16[4,16,128]{2,0,1:T(4,128)(2,1)S(1)} %all_to_all.29), channel_id=1, replica_groups=mesh['group'=2,'row'=4,'col'=4] {'group','row'}, dimensions={1}, use_global_device_ids=true | all-gather | bytes 147456 | tf_op jit(solution)/shard_map/all_gather | solution.py:108
  105.6 66.1 %while.19 = (s32[]{:T(128)}, f32[4,128,128]{1,2,0:T(8,128)}, f32[4,768,192]{1,2,0:T(8,128)S(1)}, f32[192,768]{1,0:T(8,128)}, bf16[3,128,192]{1,2,0:T(8,128)(2,1)...) while((s32[]{:T(128)}, f32[4,128,128]{1,2,0:T(8,128)}, ...), condition=%wide.region_12.13_spmd.clone, body=%wide.region_7.12_spmd.clone.sunk | while | flops 421316096 | bytes 18337588 | solution.py:195
  107.5 2.4 fusion.165
  122.5 2.2 bitcast_add_fusion.2
  129.4 2.4 fusion.165
  151.5 2.4 fusion.165
  173.5 2.3 copy.118
  175.9 3.2 convolution_bitcast_fusion
  179.1 2.3 fusion.48
  181.5 2.3 copy.110
  186.1 38.7 %all-reduce.3.cloned.1.call-done = f32[4,128,128]{2,0,1:T(4,128)} async-done(((f32[4,128,128]{2,0,1:T(4,128)}), f32[4,128,128]{2,0,1:T(4,128)}) %all-reduce.3.cloned.1.call-update) | async-done | bytes 262160
  226.6 4.6 %all-to-all-start.1 = ((f32[4,1,2048]{2,1,0:T(1,128)}), f32[4,1,2048]{2,1,0:T(1,128)S(1)}, u32[]{:S(2)}, u32[]{:S(2)}) async-start(f32[4,1,2048]{2,1,0:T(1,128)} %reshape.298), calls=%async_computation.2 | async-start | bytes 65536 | tf_op jit(solution)/shard_map/all_to_all | solution.py:221
  231.2 5.7 %all-to-all-done.1 = f32[4,1,2048]{2,1,0:T(1,128)S(1)} async-done(((f32[4,1,2048]{2,1,0:T(1,128)}), f32[4,1,2048]{2,1,0:T(1,128)S(1)}, u32[]{:S(2)}, u32[]{:S(2)}) %all-to-all-start.1) | async-done | bytes 32800 | tf_op jit(solution)/shard_map/all_to_all | solution.py:221
  238.9 31.2 %psum.14 = f32[128,16]{0,1:T(8,128)S(1)} all-reduce(f32[128,16]{0,1:T(8,128)S(1)} %convolution_bitcast_fusion.2), channel_id=1, replica_groups=mesh['group'=2,'row'=4,'col'=4] {'row','col'}, use_global_device_ids=true, to_apply=%region_16.17 | all-reduce | flops 2048 | bytes 16384 | tf_op jit(solution)/shard_map/psum | solution.py:230
  270.1 5.6 %psum.15 = f32[128,16]{0,1:T(8,128)} all-reduce(f32[128,16]{0,1:T(8,128)S(1)} %psum.14), channel_id=1, replica_groups=mesh['group'=2,'row'=4,'col'=4] {'group'}, use_global_device_ids=true, to_apply=%region_17.18 | all-reduce | flops 2048 | bytes 16384 | tf_op jit(solution)/shard_map/psum | solution.py:230
  279.0 14.8 %reduce-scatter.12.cloned.1.call-done = f32[3,32,768]{2,1,0:T(8,128)} async-done(((f32[3,128,768]{2,1,0:T(8,128)}), f32[3,32,768]{2,1,0:T(8,128)}) %reduce-scatter.12.cloned.1.call-update) | async-done | bytes 294928 | tf_op jit(solution)/shard_map/reduce_scatter | solution.py:207
  295.0 29.0 %reduce-scatter.10.cloned.1.call-done = f32[3,32,768]{2,1,0:T(8,128)} async-done(((f32[3,128,768]{2,1,0:T(8,128)}), f32[3,32,768]{2,1,0:T(8,128)}) %reduce-scatter.10.cloned.1.call-update) | async-done | bytes 294928 | tf_op jit(solution)/shard_map/reduce_scatter | solution.py:206
  326.0 46.6 %reduce-scatter.14.cloned.1.call-done = f32[4,96,192]{2,1,0:T(8,128)} async-done(((f32[4,768,192]{2,1,0:T(8,128)}), f32[4,96,192]{2,1,0:T(8,128)}) %reduce-scatter.14.cloned.1.call-update) | async-done | bytes 294928 | tf_op jit(solution)/shard_map/reduce_scatter | solution.py:219
  (200 shorter events, 86.0 us)
Async XLA Ops:
  7.2 77.1 %copy-start = (bf16[128,128]{1,0:T(8,128)(2,1)S(1)}, bf16[128,128]{1,0:T(8,128)(2,1)}, u32[]{:S(2)}) copy-start(bf16[128,128]{1,0:T(8,128)(2,1)} %param.26) | copy-start | bytes 98308
  7.2 32.5 %all-gather.2.cloned.1.call-start = ((), (), s32[]{:S(2)}) async-start(), calls=%async_computation.7 | async-start | bytes 1179648 | tf_op jit(solution)/shard_map/all_gather | solution.py:86
  13.5 67.1 %reduce-scatter.8.cloned.1.call-start = ((), (), s32[]{:S(2)}) async-start(), calls=%async_computation.8 | async-start | bytes 1310720 | tf_op jit(solution)/shard_map/reduce_scatter | solution.py:90
  51.4 31.7 %copy-start.15 = (f32[128]{0:T(128)S(1)}, f32[128]{0:T(128)}, u32[]{:S(2)}) copy-start(f32[128]{0:T(128)} %param.25) | copy-start | bytes 1540
  51.4 32.9 %copy-start.7 = (bf16[16,32,128]{2,1,0:T(8,128)(2,1)S(1)}, bf16[16,32,128]{2,1,0:T(8,128)(2,1)}, u32[]{:S(2)}) copy-start(bf16[16,32,128]{2,1,0:T(8,128)(2,1)} %param.19) | copy-start | bytes 393220
  53.1 32.3 %copy-start.11 = (bf16[128,16]{0,1:T(8,128)(2,1)S(1)}, bf16[128,16]{0,1:T(8,128)(2,1)}, u32[]{:S(2)}) copy-start(bf16[128,16]{0,1:T(8,128)(2,1)} %param.28) | copy-start | bytes 12292
  53.1 32.3 %copy-start.13 = (f32[128]{0:T(128)S(1)}, f32[128]{0:T(128)}, u32[]{:S(2)}) copy-start(f32[128]{0:T(128)} %param.27) | copy-start | bytes 1540
  53.1 32.3 %copy-start.18 = (f32[16]{0:T(128)S(1)}, f32[16]{0:T(128)}, u32[]{:S(2)}) copy-start(f32[16]{0:T(128)} %param.29) | copy-start | bytes 196
  53.1 36.7 %copy-start.19 = (s32[3]{0:T(128)S(1)}, s32[3]{0:T(128)}, u32[]{:S(2)}) copy-start(s32[3]{0:T(128)} %param.31) | copy-start | bytes 40
  53.3 52.2 %copy-start.1 = (bf16[3,128,768]{2,1,0:T(8,128)(2,1)S(1)}, bf16[3,128,768]{2,1,0:T(8,128)(2,1)}, u32[]{:S(2)}) copy-start(bf16[3,128,768]{2,1,0:T(8,128)(2,1)} %param.30) | copy-start | bytes 1769476
  53.3 52.2 %copy-start.9 = (f32[768]{0:T(1024)S(1)}, f32[768]{0:T(1024)}, u32[]{:S(2)}) copy-start(f32[768]{0:T(1024)} %param.32) | copy-start | bytes 9220
  86.5 8.8 %all-to-all-start = ((bf16[4,2,1024]{2,1,0:T(2,128)(2,1)}), bf16[4,2,1024]{2,1,0:T(2,128)(2,1)S(1)}, u32[]{:S(2)}, u32[]{:S(2)}) async-start(bf16[4,2,1024]{2,1,0:T(2,128)(2,1)} %reshape.296), calls=%async_computation.1 | async-start | bytes 32768 | tf_op jit(solution)/shard_map/all_to_all | solution.py:107
  89.7 135.1 %all-reduce.3.cloned.1.call-start = ((), (), s32[]{:S(2)}) async-start(), calls=%async_computation.13 | async-start | bytes 524288
  105.6 4.4 %copy-start.4 = (f32[4,128,128]{1,2,0:T(8,128)S(1)}, f32[4,128,128]{1,2,0:T(8,128)}, u32[]{:S(2)}) copy-start(f32[4,128,128]{1,2,0:T(8,128)} %get-tuple-element.359) | copy-start | bytes 786436 | tf_op jit(solution)/shard_map/while
  127.4 4.4 %copy-start.4 = (f32[4,128,128]{1,2,0:T(8,128)S(1)}, f32[4,128,128]{1,2,0:T(8,128)}, u32[]{:S(2)}) copy-start(f32[4,128,128]{1,2,0:T(8,128)} %get-tuple-element.359) | copy-start | bytes 786436 | tf_op jit(solution)/shard_map/while
  149.5 4.4 %copy-start.4 = (f32[4,128,128]{1,2,0:T(8,128)S(1)}, f32[4,128,128]{1,2,0:T(8,128)}, u32[]{:S(2)}) copy-start(f32[4,128,128]{1,2,0:T(8,128)} %get-tuple-element.359) | copy-start | bytes 786436 | tf_op jit(solution)/shard_map/while
  173.5 103.9 %reduce-scatter.16.cloned.1.call-start = ((), (), s32[]{:S(2)}) async-start(), calls=%async_computation.12 | async-start | bytes 884736
  175.8 118.0 %reduce-scatter.12.cloned.1.call-start = ((), (), s32[]{:S(2)}) async-start(), calls=%async_computation.10 | async-start | bytes 1474560 | tf_op jit(solution)/shard_map/reduce_scatter | solution.py:207
  179.1 144.9 %reduce-scatter.10.cloned.1.call-start = ((), (), s32[]{:S(2)}) async-start(), calls=%async_computation.9 | async-start | bytes 1474560 | tf_op jit(solution)/shard_map/reduce_scatter | solution.py:206
  181.5 191.1 %reduce-scatter.14.cloned.1.call-start = ((), (), s32[]{:S(2)}) async-start(), calls=%async_computation.11 | async-start | bytes 3538944 | tf_op jit(solution)/shard_map/reduce_scatter | solution.py:219
  183.8 54.7 %copy-start.6 = (f32[16,32,128]{2,1,0:T(8,128)S(1)}, f32[16,32,128]{2,1,0:T(8,128)}, u32[]{:S(2)}) copy-start(f32[16,32,128]{2,1,0:T(8,128)} %copy-done.5) | copy-start | bytes 786436
  183.8 54.7 %copy-start.14 = (f32[128]{0:T(128)S(1)}, f32[128]{0:T(128)}, u32[]{:S(2)}) copy-start(f32[128]{0:T(128)} %param.27) | copy-start | bytes 1540
  183.8 91.9 %copy-start.12 = (bf16[128,16]{0,1:T(8,128)(2,1)S(1)}, bf16[128,16]{0,1:T(8,128)(2,1)}, u32[]{:S(2)}) copy-start(bf16[128,16]{0,1:T(8,128)(2,1)} %param.28) | copy-start | bytes 12292
  226.6 10.3 %all-to-all-start.1 = ((f32[4,1,2048]{2,1,0:T(1,128)}), f32[4,1,2048]{2,1,0:T(1,128)S(1)}, u32[]{:S(2)}, u32[]{:S(2)}) async-start(f32[4,1,2048]{2,1,0:T(1,128)} %reshape.298), calls=%async_computation.2 | async-start | bytes 65536 | tf_op jit(solution)/shard_map/all_to_all | solution.py:221
  (14 other events, 25.5 us)
Sparse Core Ops, SparseCore 0:
  13.6 26.0 all-gather.1
  53.2 27.2 reduce-scatter.7
  173.6 51.1 all-reduce.2
  227.8 34.4 reduce-scatter.15
  264.5 29.2 reduce-scatter.11
  296.0 27.9 reduce-scatter.9
  327.9 44.6 reduce-scatter.13
